TPU v7x, 256 devices: a whole 4x4x8 slice. The times are simulated.
256 devices in a mesh: leaf: 64 (over z, y, core), front: 4 (over x).
Axes of the slice: x: 4, y: 4, z: 8, core: 2. Of those that a mesh axis runs over, the one named last changes fastest.
Arguments:
- rhs_leaf: float32 [32, 65536], P(None, ('leaf', 'front')), may hold values from -6 to 6
- rhs_sep: float32 [32, 32768], P(None, ('leaf', 'front')), may hold values from -6 to 6
- inv_leaf: float32 [64, 1024, 1024], P('leaf', 'front'), may hold values from -0.1875 to 0.1875
- inv_sep: float32 [64, 512, 512], P('leaf', 'front'), may hold values from -0.25 to 0.25
- push_leaf: float32 [64, 128, 1024], P('leaf', None, 'front'), may hold values from -0.09375 to 0.09375
- push_sep: float32 [64, 128, 512], P('leaf', None, 'front'), may hold values from -0.125 to 0.125
- pull_leaf: float32 [64, 1024, 128], P('leaf', 'front'), may hold values from -0.25 to 0.25
- pull_sep: float32 [64, 512, 128], P('leaf', 'front'), may hold values from -0.25 to 0.25
- rows_leaf: int32 [64, 128], P('leaf'), may hold values from 0 to 511, as said below
- rows_sep: int32 [64, 128], P('leaf'), may hold values from 0 to 511, as said below
- pivot_leaf: int32 [64, 1024], P('leaf'), may hold values from 0 to 1023, each once within a row
- pivot_sep: int32 [64, 512], P('leaf'), may hold values from 0 to 511, each once within a row
- basis_leaf: float32 [50, 65536], P(None, ('leaf', 'front')), may hold values from -6 to 6
- basis_sep: float32 [50, 32768], P(None, ('leaf', 'front')), may hold values from -6 to 6
Outputs:
- q_leaf: float32 [32, 65536], P(None, ('leaf', 'front'))
- q_sep: float32 [32, 32768], P(None, ('leaf', 'front'))
- coeffs: float32 [50, 32], replicated
- rfac: float32 [32, 32], replicated
Inputs may be any that keep to these rules, and one draw needn't show every extreme that they name: `rows_leaf`: each row holds 128 different rows of a separator front. `rows_sep`: each row holds 128 different rows of a separator front. `pivot_leaf`: each row is a permutation. `pivot_sep`: each row is a permutation.
All inputs are finite; a program needn't handle non-finite values.
Results may differ from a plain program's by a relative error of at most 0.0001.
Values sent between devices are 32-bit elements; how exact they have to be, the bound alone decides.
A program may use at most 64 MiB of HBM per device.

v0:
```python
import functools

import jax
import jax.numpy as jnp
from jax import lax
from jax.sharding import Mesh
from jax.sharding import PartitionSpec as P

LEAF = ("leaf_0", "leaf_1", "leaf_2")
LEAF_FRONT = ("leaf_0", "leaf_1", "leaf_2", "front")


exact_mode = lax.Precision.HIGHEST


def cut_along(array, dim, length):
    lengths = array.shape
    pieces = array.reshape(*lengths[:dim], length, lengths[dim] // length, *lengths[dim + 1 :])
    return jnp.moveaxis(pieces, dim, 0)


def sum_at_owner(array, axis, dim):
    pieces = cut_along(array, dim, lax.axis_size(axis))
    arrived = lax.all_to_all(pieces, axis, split_axis=0, concat_axis=0, tiled=True)
    return arrived.sum(axis=0)


def joined_along(pieces, dim):
    pieces = jnp.moveaxis(pieces, 0, dim)
    lengths = pieces.shape
    return pieces.reshape(*lengths[:dim], lengths[dim] * lengths[dim + 1], *lengths[dim + 2 :])


def from_everyone(array, axis):
    copies = jnp.broadcast_to(array, (lax.axis_size(axis), *array.shape))
    return lax.all_to_all(copies, axis, split_axis=0, concat_axis=0, tiled=True)


def gathered_copies(array, axis, dim):
    return joined_along(from_everyone(array, axis), dim)


def rows_first(arrays, axis, dims):
    turned = [jnp.moveaxis(a, dim, 0) for a, dim in zip(arrays, dims)]
    widths = [t[0].size for t in turned]
    both = jnp.concatenate([t.reshape(-1, w) for t, w in zip(turned, widths)], axis=1)
    whole = lax.all_gather(both, axis, axis=0, tiled=True)
    pieces = jnp.split(whole, [sum(widths[:k]) for k in range(1, len(widths))], axis=1)
    return tuple(
        (
            jnp.moveaxis(b.reshape(-1, *t.shape[1:]), 0, dim)
            for b, t, dim in zip(pieces, turned, dims)
        )
    )


def by_axis(array, axes):
    return functools.reduce(lax.psum, axes, array)


def contract(former, latter):
    return lax.dot_general(
        former,
        latter,
        (((1,), (1,)), ((), ())),
        precision=exact_mode,
        preferred_element_type=jnp.float32,
    )


def expand(coeff_block, basis):
    return jnp.dot(coeff_block.T, basis, precision=exact_mode, preferred_element_type=jnp.float32)


def apply_inverse(gathered, inverse, pivots):
    return contract(gathered[:, pivots], inverse)


def solve_if(active, gathered, inverse, pivots):

    def chosen(operand):
        return apply_inverse(operand, inverse, pivots)

    def skipped(operand):
        return jnp.zeros((operand.shape[0], inverse.shape[0]), jnp.float32)

    return lax.cond(active, chosen, skipped, gathered)


def pick_piece(pool, index, valid):
    safe = jnp.clip(index, 0, pool.shape[0] - 1)
    piece = lax.dynamic_index_in_dim(pool, safe, 0, keepdims=False)
    return jnp.where(valid, piece, jnp.zeros_like(piece))


def push_compact(state, weights):
    return sum_at_owner(contract(state, weights), "front", 1)


def sep_gathered(shares):
    return gathered_copies(shares, "front", 1)


def leaf_gathered(shares):
    return gathered_copies(shares, "front", 1)


def on_device(
    rhs_leaf,
    rhs_sep,
    inv_leaf,
    inv_sep,
    push_leaf,
    push_sep,
    pull_leaf,
    pull_sep,
    rows_leaf,
    rows_sep,
    pivot_leaf,
    pivot_sep,
    basis_leaf,
    basis_sep,
):
    holder = lax.axis_index(LEAF)
    groups = lax.axis_size(LEAF)
    top_level = groups.bit_length() - 1
    sep_width = pivot_sep.shape[1]
    share_width = rhs_sep.shape[1]
    leaf_inverse = inv_leaf[0]
    sep_inverse = inv_sep[0]
    leaf_pivots = pivot_leaf[0]
    sep_pivots = pivot_sep[0]
    level_of = jnp.full((), top_level + 1, jnp.int32)
    for bit_index in range(top_level, 0, -1):
        level_of = jnp.where(holder % 2**bit_index != 0, jnp.int32(bit_index), level_of)
    leaf_state = apply_inverse(leaf_gathered(rhs_leaf), leaf_inverse, leaf_pivots)
    sep_state = jnp.zeros_like(rhs_sep)
    leaf_compact = push_compact(leaf_state, push_leaf[0])
    sep_compact = jnp.zeros_like(leaf_compact)
    front_start = lax.axis_index("front") * share_width
    for height in range(1, top_level + 2):
        if height == 1:
            lower_index = holder - 1
            upper_index = holder
        else:
            lower_index = holder - 2 ** (height - 2)
            upper_index = holder + 2 ** (height - 2)
        lower_valid = jnp.logical_and(lower_index >= 0, height <= top_level)
        upper_valid = upper_index < groups
        source = leaf_compact if height == 1 else sep_compact
        source_rows = rows_leaf[0] if height == 1 else rows_sep[0]
        pool, pool_rows = (
            gathered_copies(source[None], LEAF, 0),
            gathered_copies(source_rows[None], LEAF, 0),
        )
        first_part = pick_piece(pool, upper_index, upper_valid)
        first_rows = pick_piece(pool_rows, upper_index, upper_valid)
        second_part = pick_piece(pool, lower_index, lower_valid)
        second_rows = pick_piece(pool_rows, lower_index, lower_valid)
        first_full, second_full = rows_first((first_part, second_part), "front", (1, 1))
        dense = jnp.zeros((rhs_sep.shape[0], sep_width), jnp.float32)
        dense = dense.at[:, first_rows].add(first_full).at[:, second_rows].add(second_full)
        arriving = lax.dynamic_slice_in_dim(dense, front_start, share_width, 1)
        active = level_of == height
        applied = solve_if(active, sep_gathered(rhs_sep - arriving), sep_inverse, sep_pivots)
        sep_state = jnp.where(active, applied, sep_state)
        if height <= top_level:
            sep_compact = jnp.where(active, push_compact(sep_state, push_sep[0]), sep_compact)
    sep_solution = sep_state
    leaf_solution = leaf_state
    for height in range(top_level, -1, -1):
        if height == top_level:
            parent_index = jnp.zeros((), jnp.int32)
        elif height >= 1:
            parent_index = (2 * (holder // 2 ** (height + 1)) + 1) * 2**height
        else:
            parent_index = holder // 2 * 2 + 1
        pool = gathered_copies(sep_solution[None], LEAF, 0)
        picked = lax.dynamic_index_in_dim(pool, parent_index, 0, keepdims=False)
        parent = gathered_copies(picked, "front", 1)
        if height >= 1:
            lifted = contract(parent[:, rows_sep[0]], pull_sep[0])
            active = level_of == height
            applied = solve_if(active, sep_gathered(lifted), sep_inverse, sep_pivots)
            sep_solution = jnp.where(active, sep_state - applied, sep_solution)
        else:
            lifted = contract(parent[:, rows_leaf[0]], pull_leaf[0])
            leaf_solution = leaf_state - apply_inverse(
                leaf_gathered(lifted), leaf_inverse, leaf_pivots
            )
    total_rows = groups * (pivot_leaf.shape[1] + sep_width)
    first_sum, metric_sum = (
        by_axis(
            contract(basis_leaf, leaf_solution) + contract(basis_sep, sep_solution), LEAF_FRONT
        ),
        by_axis(contract(basis_leaf, basis_leaf) + contract(basis_sep, basis_sep), LEAF_FRONT),
    )
    first_proj = first_sum / total_rows
    metric = metric_sum / total_rows
    once_leaf = leaf_solution - expand(first_proj, basis_leaf)
    once_sep = sep_solution - expand(first_proj, basis_sep)
    second_sum, self_sum = (
        by_axis(contract(basis_leaf, once_leaf) + contract(basis_sep, once_sep), LEAF_FRONT),
        by_axis(contract(once_leaf, once_leaf) + contract(once_sep, once_sep), LEAF_FRONT),
    )
    second = second_sum / total_rows
    twice_leaf = once_leaf - expand(second, basis_leaf)
    twice_sep = once_sep - expand(second, basis_sep)
    cross = jnp.dot(second.T, second, precision=exact_mode, preferred_element_type=jnp.float32)
    curved = jnp.dot(
        second.T,
        jnp.dot(metric, second, precision=exact_mode, preferred_element_type=jnp.float32),
        precision=exact_mode,
        preferred_element_type=jnp.float32,
    )
    gram_matrix = self_sum / total_rows - 2.0 * cross + curved
    lower_factor = jnp.linalg.cholesky(gram_matrix)
    q_leaf = lax.linalg.triangular_solve(lower_factor, twice_leaf, left_side=True, lower=True)
    q_sep = lax.linalg.triangular_solve(lower_factor, twice_sep, left_side=True, lower=True)
    return (q_leaf, q_sep, first_proj + second, lower_factor.T)


def solution(mesh):
    torus = Mesh(
        mesh.devices.reshape(8, 4, 2, mesh.shape["front"]), ("leaf_0", "leaf_1", "leaf_2", "front")
    )
    return jax.shard_map(
        on_device,
        mesh=torus,
        in_specs=(
            P(None, LEAF_FRONT),
            P(None, LEAF_FRONT),
            P(LEAF, "front", None),
            P(LEAF, "front", None),
            P(LEAF, None, "front"),
            P(LEAF, None, "front"),
            P(LEAF, "front", None),
            P(LEAF, "front", None),
            P(LEAF, None),
            P(LEAF, None),
            P(LEAF, None),
            P(LEAF, None),
            P(None, LEAF_FRONT),
            P(None, LEAF_FRONT),
        ),
        out_specs=(P(None, LEAF_FRONT), P(None, LEAF_FRONT), P(), P()),
        check_vma=False,
    )
```

profile of v0, /device:TPU:1, one launch (start us, length us, event | category | flops | bytes accessed | tf_op | source)
XLA Modules:
  0.0 962.2 jit_solution(1290878768696683510)
XLA Ops:
  24.3 14.9 %all-to-all-start.2 = ((s32[64,1,128]{2,1,0:T(1,128)}), s32[64,1,128]{2,1,0:T(1,128)S(1)}, u32[]{:S(2)}, u32[]{:S(2)}) async-start(s32[64,1,128]{2,1,0:T(1,128)} %broadcast_in_dim.199), calls=%async_computation.2 | async-start | bytes 65536 | tf_op jit(solution)/shard_map/all_to_all | solution.py:36
  53.3 13.1 %all-to-all-done.4 = f32[64,1,1024]{2,1,0:T(1,128)S(1)} async-done(((f32[64,1,1024]{2,1,0:T(1,128)}), f32[64,1,1024]{2,1,0:T(1,128)S(1)}, u32[]{:S(2)}, u32[]{:S(2)}) %all-to-all-start.4) | async-done | bytes 262176 | tf_op jit(solution)/shard_map/all_to_all | solution.py:36
  99.6 9.1 all-to-all-start.1
  122.8 13.1 %all-to-all-done.7 = f32[64,1,1024]{2,1,0:T(1,128)S(1)} async-done(((f32[64,1,1024]{2,1,0:T(1,128)}), f32[64,1,1024]{2,1,0:T(1,128)S(1)}, u32[]{:S(2)}, u32[]{:S(2)}) %all-to-all-start.7) | async-done | bytes 262176 | tf_op jit(solution)/shard_map/all_to_all | solution.py:36
  137.6 9.2 all_gather.22
  166.3 24.6 %all_to_all.233 = f32[64,1,1024]{2,1,0:T(1,128)S(1)} all-to-all(f32[64,1,1024]{2,1,0:T(1,128)S(1)} %reshape.976), channel_id=1, replica_groups=mesh['leaf_0'=8,'leaf_1'=4,'leaf_2'=2,'front'=4] {'leaf_0','leaf_1','lea..., dimensions={0} | all-to-all | bytes 524288 | tf_op jit(solution)/shard_map/all_to_all | solution.py:36
  221.4 24.4 %all_to_all.235 = f32[64,1,1024]{2,1,0:T(1,128)S(1)} all-to-all(f32[64,1,1024]{2,1,0:T(1,128)S(1)} %reshape.980), channel_id=1, replica_groups=mesh['leaf_0'=8,'leaf_1'=4,'leaf_2'=2,'front'=4] {'leaf_0','leaf_1','lea..., dimensions={0} | all-to-all | bytes 524288 | tf_op jit(solution)/shard_map/all_to_all | solution.py:36
  277.4 10.9 %all-to-all-start.16 = ((f32[64,1,1024]{2,1,0:T(1,128)}), f32[64,1,1024]{2,1,0:T(1,128)S(1)}, u32[]{:S(2)}, u32[]{:S(2)}) async-start(f32[64,1,1024]{2,1,0:T(1,128)} %reshape.984), calls=%async_computation.16 | async-start | bytes 524288 | tf_op jit(solution)/shard_map/all_to_all | solution.py:36
  288.3 13.0 %all-to-all-done.16 = f32[64,1,1024]{2,1,0:T(1,128)S(1)} async-done(((f32[64,1,1024]{2,1,0:T(1,128)}), f32[64,1,1024]{2,1,0:T(1,128)S(1)}, u32[]{:S(2)}, u32[]{:S(2)}) %all-to-all-start.16) | async-done | bytes 262176 | tf_op jit(solution)/shard_map/all_to_all | solution.py:36
  331.8 23.6 %all_to_all.238 = f32[64,1,1024]{2,1,0:T(1,128)S(1)} all-to-all(f32[64,1,1024]{2,1,0:T(1,128)S(1)} %reshape.988), channel_id=1, replica_groups=mesh['leaf_0'=8,'leaf_1'=4,'leaf_2'=2,'front'=4] {'leaf_0','leaf_1','lea..., dimensions={0} | all-to-all | bytes 524288 | tf_op jit(solution)/shard_map/all_to_all | solution.py:36
  385.9 23.8 %all_to_all.240 = f32[64,1,1024]{2,1,0:T(1,128)S(1)} all-to-all(f32[64,1,1024]{2,1,0:T(1,128)S(1)} %reshape.992), channel_id=1, replica_groups=mesh['leaf_0'=8,'leaf_1'=4,'leaf_2'=2,'front'=4] {'leaf_0','leaf_1','lea..., dimensions={0} | all-to-all | bytes 524288 | tf_op jit(solution)/shard_map/all_to_all | solution.py:36
  432.6 10.2 %all-to-all-start.24 = ((f32[64,1,32,128]{3,2,1,0:T(8,128)}), f32[64,1,32,128]{3,2,1,0:T(8,128)S(1)}, u32[]{:S(2)}, u32[]{:S(2)}) async-start(f32[64,1,32,128]{3,2,1,0:T(8,128)} %broadcast_in_dim.214), calls=%async_computation.24 | async-start | bytes 2097152 | tf_op jit(solution)/shard_map/all_to_all | solution.py:36
  442.8 28.3 %all-to-all-done.24 = f32[64,1,32,128]{3,2,1,0:T(8,128)S(1)} async-done(((f32[64,1,32,128]{3,2,1,0:T(8,128)}), f32[64,1,32,128]{3,2,1,0:T(8,128)S(1)}, u32[]{:S(2)}, u32[]{:S(2)}) %all-to-all-start.24) | async-done | bytes 1048608 | tf_op jit(solution)/shard_map/all_to_all | solution.py:36
  490.2 9.1 all-to-all-start.27
  499.3 28.1 %all-to-all-done.27 = f32[64,1,32,128]{3,2,1,0:T(8,128)S(1)} async-done(((f32[64,1,32,128]{3,2,1,0:T(8,128)}), f32[64,1,32,128]{3,2,1,0:T(8,128)S(1)}, u32[]{:S(2)}, u32[]{:S(2)}) %all-to-all-start.27) | async-done | bytes 1048608 | tf_op jit(solution)/shard_map/all_to_all | solution.py:36
  544.8 9.2 all-to-all-start.30
  554.0 28.2 %all-to-all-done.30 = f32[64,1,32,128]{3,2,1,0:T(8,128)S(1)} async-done(((f32[64,1,32,128]{3,2,1,0:T(8,128)}), f32[64,1,32,128]{3,2,1,0:T(8,128)S(1)}, u32[]{:S(2)}, u32[]{:S(2)}) %all-to-all-start.30) | async-done | bytes 1048608 | tf_op jit(solution)/shard_map/all_to_all | solution.py:36
  599.5 9.7 %all-to-all-start.33 = ((f32[64,1,32,128]{3,2,1,0:T(8,128)}), f32[64,1,32,128]{3,2,1,0:T(8,128)S(1)}, u32[]{:S(2)}, u32[]{:S(2)}) async-start(f32[64,1,32,128]{3,2,1,0:T(8,128)} %broadcast_in_dim.223), calls=%async_computation.33 | async-start | bytes 2097152 | tf_op jit(solution)/shard_map/all_to_all | solution.py:36
  609.3 28.2 %all-to-all-done.33 = f32[64,1,32,128]{3,2,1,0:T(8,128)S(1)} async-done(((f32[64,1,32,128]{3,2,1,0:T(8,128)}), f32[64,1,32,128]{3,2,1,0:T(8,128)S(1)}, u32[]{:S(2)}, u32[]{:S(2)}) %all-to-all-start.33) | async-done | bytes 1048608 | tf_op jit(solution)/shard_map/all_to_all | solution.py:36
  654.8 10.1 %all-to-all-start.36 = ((f32[64,1,32,128]{3,2,1,0:T(8,128)}), f32[64,1,32,128]{3,2,1,0:T(8,128)S(1)}, u32[]{:S(2)}, u32[]{:S(2)}) async-start(f32[64,1,32,128]{3,2,1,0:T(8,128)} %broadcast_in_dim.226), calls=%async_computation.36 | async-start | bytes 2097152 | tf_op jit(solution)/shard_map/all_to_all | solution.py:36
  665.0 28.2 %all-to-all-done.36 = f32[64,1,32,128]{3,2,1,0:T(8,128)S(1)} async-done(((f32[64,1,32,128]{3,2,1,0:T(8,128)}), f32[64,1,32,128]{3,2,1,0:T(8,128)S(1)}, u32[]{:S(2)}, u32[]{:S(2)}) %all-to-all-start.36) | async-done | bytes 1048608 | tf_op jit(solution)/shard_map/all_to_all | solution.py:36
  710.5 10.3 %all-to-all-start.39 = ((f32[64,1,32,128]{3,2,1,0:T(8,128)}), f32[64,1,32,128]{3,2,1,0:T(8,128)S(1)}, u32[]{:S(2)}, u32[]{:S(2)}) async-start(f32[64,1,32,128]{3,2,1,0:T(8,128)} %broadcast_in_dim.229), calls=%async_computation.39 | async-start | bytes 2097152 | tf_op jit(solution)/shard_map/all_to_all | solution.py:36
  720.9 28.2 %all-to-all-done.39 = f32[64,1,32,128]{3,2,1,0:T(8,128)S(1)} async-done(((f32[64,1,32,128]{3,2,1,0:T(8,128)}), f32[64,1,32,128]{3,2,1,0:T(8,128)S(1)}, u32[]{:S(2)}, u32[]{:S(2)}) %all-to-all-start.39) | async-done | bytes 1048608 | tf_op jit(solution)/shard_map/all_to_all | solution.py:36
  775.3 27.9 %all-to-all-done.42 = f32[64,1,32,128]{3,2,1,0:T(8,128)S(1)} async-done(((f32[64,1,32,128]{3,2,1,0:T(8,128)}), f32[64,1,32,128]{3,2,1,0:T(8,128)S(1)}, u32[]{:S(2)}, u32[]{:S(2)}) %all-to-all-start.42) | async-done | bytes 1048608 | tf_op jit(solution)/shard_map/all_to_all | solution.py:36
  826.1 21.6 %psum.112 = f32[50,32]{0,1:T(8,128)S(1)} all-reduce(f32[50,32]{0,1:T(8,128)S(1)} %fusion.2), channel_id=1, replica_groups=mesh['leaf_0'=8,'leaf_1'=4,'leaf_2'=2,'front'=4] {'leaf_0'}, use_global_device_ids=true, to_apply=%region_47.48 | all-reduce | flops 1600 | bytes 12800 | tf_op jit(solution)/shard_map/psum | solution.py:58
  847.7 12.4 %psum.113 = f32[50,32]{0,1:T(8,128)S(1)} all-reduce(f32[50,32]{0,1:T(8,128)S(1)} %psum.112), channel_id=1, replica_groups=mesh['leaf_0'=8,'leaf_1'=4,'leaf_2'=2,'front'=4] {'leaf_1'}, use_global_device_ids=true, to_apply=%region_48.49 | all-reduce | flops 1600 | bytes 12800 | tf_op jit(solution)/shard_map/psum | solution.py:58
  860.1 17.0 %psum.114 = f32[50,32]{0,1:T(8,128)S(1)} all-reduce(f32[50,32]{0,1:T(8,128)S(1)} %psum.113), channel_id=1, replica_groups=mesh['leaf_0'=8,'leaf_1'=4,'leaf_2'=2,'front'=4] {'leaf_2'}, use_global_device_ids=true, to_apply=%region_49.50 | all-reduce | flops 1600 | bytes 12800 | tf_op jit(solution)/shard_map/psum | solution.py:58
  877.1 11.5 %psum.115 = f32[50,32]{0,1:T(8,128)S(1)} all-reduce(f32[50,32]{0,1:T(8,128)S(1)} %psum.114), channel_id=1, replica_groups=mesh['leaf_0'=8,'leaf_1'=4,'leaf_2'=2,'front'=4] {'front'}, use_global_device_ids=true, to_apply=%region_50.51 | all-reduce | flops 1600 | bytes 12800 | tf_op jit(solution)/shard_map/psum | solution.py:58
  889.6 20.6 %all-reduce.1 = (f32[50,32]{0,1:T(8,128)S(1)}, f32[32,32]{0,1:T(8,128)S(1)}, f32[50,50]{1,0:T(8,128)S(1)}) all-reduce(f32[50,32]{0,1:T(8,128)S(1)} %fusion.1, f32[32,32]{0,1:T(8,128)S(1)} %convolution_add_fusion.3, f32[50,50]{1,0:T(8,128)S(1)} %convolution_add_fusion), channel_id=1, replica_groups=mesh['leaf_0'=8,'leaf_1'=4,'leaf_2'=2,'front'=4] {'leaf_0'}, use_global_device_ids=true, to_apply=%region_55.56 | all-reduce | flops 5124 | bytes 40992 | tf_op jit(solution)/shard_map/psum | solution.py:58
  910.2 11.4 %all-reduce.3 = (f32[50,32]{0,1:T(8,128)S(1)}, f32[32,32]{0,1:T(8,128)S(1)}, f32[50,50]{1,0:T(8,128)S(1)}) all-reduce(f32[50,32]{0,1:T(8,128)S(1)} %get-tuple-element.267, f32[32,32]{0,1:T(8,128)S(1)} %get-tuple-element.268, f32[50,50]{1,0:T(8,128)S(1)} %get-tuple-element.269), channel_id=1, replica_groups=mesh['leaf_0'=8,'leaf_1'=4,'leaf_2'=2,'front'=4] {'leaf_1'}, use_global_device_ids=true, to_apply=%region_56.57 | all-reduce | flops 5124 | bytes 40992 | tf_op jit(solution)/shard_map/psum | solution.py:58
  921.6 17.9 %all-reduce.4 = (f32[50,32]{0,1:T(8,128)S(1)}, f32[32,32]{0,1:T(8,128)S(1)}, f32[50,50]{1,0:T(8,128)S(1)}) all-reduce(f32[50,32]{0,1:T(8,128)S(1)} %get-tuple-element.273, f32[32,32]{0,1:T(8,128)S(1)} %get-tuple-element.274, f32[50,50]{1,0:T(8,128)S(1)} %get-tuple-element.275), channel_id=1, replica_groups=mesh['leaf_0'=8,'leaf_1'=4,'leaf_2'=2,'front'=4] {'leaf_2'}, use_global_device_ids=true, to_apply=%region_57.58 | all-reduce | flops 5124 | bytes 40992 | tf_op jit(solution)/shard_map/psum | solution.py:58
  939.5 11.8 %all-reduce.2 = (f32[50,32]{0,1:T(8,128)S(1)}, f32[32,32]{0,1:T(8,128)S(1)}, f32[50,50]{1,0:T(8,128)S(1)}) all-reduce(f32[50,32]{0,1:T(8,128)S(1)} %get-tuple-element.276, f32[32,32]{0,1:T(8,128)S(1)} %get-tuple-element.277, f32[50,50]{1,0:T(8,128)S(1)} %get-tuple-element.278), channel_id=1, replica_groups=mesh['leaf_0'=8,'leaf_1'=4,'leaf_2'=2,'front'=4] {'front'}, use_global_device_ids=true, to_apply=%region_58.59 | all-reduce | flops 5124 | bytes 40992 | tf_op jit(solution)/shard_map/psum | solution.py:58
  (353 shorter events, 403.5 us)
Async XLA Ops:
  0.6 14.3 %copy-start = (f32[1,256,1024]{2,1,0:T(8,128)S(1)}, f32[1,256,1024]{2,1,0:T(8,128)}, u32[]{:S(2)}) copy-start(f32[1,256,1024]{2,1,0:T(8,128)} %param.42) | copy-start | bytes 3145732
  2.1 9.8 %all-to-all-start = ((f32[4,32,256]{2,1,0:T(8,128)}), f32[4,32,256]{2,1,0:T(8,128)S(1)}, u32[]{:S(2)}, u32[]{:S(2)}) async-start(f32[4,32,256]{2,1,0:T(8,128)} %broadcast_in_dim.197), calls=%async_computation | async-start | bytes 262144 | tf_op jit(solution)/shard_map/all_to_all | solution.py:36
  24.3 24.2 %all-to-all-start.2 = ((s32[64,1,128]{2,1,0:T(1,128)}), s32[64,1,128]{2,1,0:T(1,128)S(1)}, u32[]{:S(2)}, u32[]{:S(2)}) async-start(s32[64,1,128]{2,1,0:T(1,128)} %broadcast_in_dim.199), calls=%async_computation.2 | async-start | bytes 65536 | tf_op jit(solution)/shard_map/all_to_all | solution.py:36
  48.6 17.9 %all-to-all-start.4 = ((f32[64,1,1024]{2,1,0:T(1,128)}), f32[64,1,1024]{2,1,0:T(1,128)S(1)}, u32[]{:S(2)}, u32[]{:S(2)}) async-start(f32[64,1,1024]{2,1,0:T(1,128)} %reshape.968), calls=%async_computation.4 | async-start | bytes 524288 | tf_op jit(solution)/shard_map/all_to_all | solution.py:36
  79.7 9.1 copy-start.1
  81.0 7.7 all-to-all-start.5
  99.6 18.4 %all-to-all-start.1 = ((s32[64,1,128]{2,1,0:T(1,128)}), s32[64,1,128]{2,1,0:T(1,128)S(1)}, u32[]{:S(2)}, u32[]{:S(2)}) async-start(s32[64,1,128]{2,1,0:T(1,128)} %broadcast_in_dim.198), calls=%async_computation.1 | async-start | bytes 65536 | tf_op jit(solution)/shard_map/all_to_all | solution.py:36
  118.0 17.9 %all-to-all-start.7 = ((f32[64,1,1024]{2,1,0:T(1,128)}), f32[64,1,1024]{2,1,0:T(1,128)S(1)}, u32[]{:S(2)}, u32[]{:S(2)}) async-start(f32[64,1,1024]{2,1,0:T(1,128)} %reshape.972), calls=%async_computation.7 | async-start | bytes 524288 | tf_op jit(solution)/shard_map/all_to_all | solution.py:36
  150.0 7.7 all-to-all-start.8
  205.1 7.7 all-to-all-start.11
  260.0 7.7 all-to-all-start.14
  277.4 24.0 %all-to-all-start.16 = ((f32[64,1,1024]{2,1,0:T(1,128)}), f32[64,1,1024]{2,1,0:T(1,128)S(1)}, u32[]{:S(2)}, u32[]{:S(2)}) async-start(f32[64,1,1024]{2,1,0:T(1,128)} %reshape.984), calls=%async_computation.16 | async-start | bytes 524288 | tf_op jit(solution)/shard_map/all_to_all | solution.py:36
  315.5 7.7 all-to-all-start.17
  369.6 7.7 all-to-all-start.20
  423.8 7.7 all-to-all-start.23
  432.6 38.5 %all-to-all-start.24 = ((f32[64,1,32,128]{3,2,1,0:T(8,128)}), f32[64,1,32,128]{3,2,1,0:T(8,128)S(1)}, u32[]{:S(2)}, u32[]{:S(2)}) async-start(f32[64,1,32,128]{3,2,1,0:T(8,128)} %broadcast_in_dim.214), calls=%async_computation.24 | async-start | bytes 2097152 | tf_op jit(solution)/shard_map/all_to_all | solution.py:36
  471.7 7.7 all-to-all-start.25
  481.3 7.7 all-to-all-start.26
  490.2 37.3 %all-to-all-start.27 = ((f32[64,1,32,128]{3,2,1,0:T(8,128)}), f32[64,1,32,128]{3,2,1,0:T(8,128)S(1)}, u32[]{:S(2)}, u32[]{:S(2)}) async-start(f32[64,1,32,128]{3,2,1,0:T(8,128)} %broadcast_in_dim.217), calls=%async_computation.27 | async-start | bytes 2097152 | tf_op jit(solution)/shard_map/all_to_all | solution.py:36
  536.0 7.7 all-to-all-start.29
  544.8 37.3 %all-to-all-start.30 = ((f32[64,1,32,128]{3,2,1,0:T(8,128)}), f32[64,1,32,128]{3,2,1,0:T(8,128)S(1)}, u32[]{:S(2)}, u32[]{:S(2)}) async-start(f32[64,1,32,128]{3,2,1,0:T(8,128)} %broadcast_in_dim.220), calls=%async_computation.30 | async-start | bytes 2097152 | tf_op jit(solution)/shard_map/all_to_all | solution.py:36
  590.7 7.7 all-to-all-start.32
  599.5 37.9 %all-to-all-start.33 = ((f32[64,1,32,128]{3,2,1,0:T(8,128)}), f32[64,1,32,128]{3,2,1,0:T(8,128)S(1)}, u32[]{:S(2)}, u32[]{:S(2)}) async-start(f32[64,1,32,128]{3,2,1,0:T(8,128)} %broadcast_in_dim.223), calls=%async_computation.33 | async-start | bytes 2097152 | tf_op jit(solution)/shard_map/all_to_all | solution.py:36
  646.0 7.7 all-to-all-start.35
  654.8 38.3 %all-to-all-start.36 = ((f32[64,1,32,128]{3,2,1,0:T(8,128)}), f32[64,1,32,128]{3,2,1,0:T(8,128)S(1)}, u32[]{:S(2)}, u32[]{:S(2)}) async-start(f32[64,1,32,128]{3,2,1,0:T(8,128)} %broadcast_in_dim.226), calls=%async_computation.36 | async-start | bytes 2097152 | tf_op jit(solution)/shard_map/all_to_all | solution.py:36
  701.6 7.7 all-to-all-start.38
  710.5 38.5 %all-to-all-start.39 = ((f32[64,1,32,128]{3,2,1,0:T(8,128)}), f32[64,1,32,128]{3,2,1,0:T(8,128)S(1)}, u32[]{:S(2)}, u32[]{:S(2)}) async-start(f32[64,1,32,128]{3,2,1,0:T(8,128)} %broadcast_in_dim.229), calls=%async_computation.39 | async-start | bytes 2097152 | tf_op jit(solution)/shard_map/all_to_all | solution.py:36
  757.5 7.7 all-to-all-start.41
  768.2 7.0 copy-start.4
  768.2 35.1 %all-to-all-start.42 = ((f32[64,1,32,128]{3,2,1,0:T(8,128)}), f32[64,1,32,128]{3,2,1,0:T(8,128)S(1)}, u32[]{:S(2)}, u32[]{:S(2)}) async-start(f32[64,1,32,128]{3,2,1,0:T(8,128)} %broadcast_in_dim.232), calls=%async_computation.42 | async-start | bytes 2097152 | tf_op jit(solution)/shard_map/all_to_all | solution.py:36
  803.9 7.7 all-to-all-start.43
  813.6 8.1 all-to-all-start.44
  (10 other events, 17.5 us)
where the time goes:
time: 976 us; the launch traced here: 962 us
  blocking collectives  364 us (37%)
  waiting for transfers between devices  326 us (33%)
  starting transfers between devices  167 us (17%)
  local copies, waits for them, and re-layouts  50 us (5%)
  other arithmetic  40.6 us (4%)
  matrix products  11.6 us (1%)
    all_to_all x29, waiting for transfers between devices, from_everyone(): return lax.all_to_all(copies, axis, split_axis=0, concat_axis=0, tiled=True)  326 us
    all_to_all x29, starting transfers between devices, from_everyone(): return lax.all_to_all(copies, axis, split_axis=0, concat_axis=0, tiled=True)  167 us
    all_to_all x9, blocking collectives, from_everyone(): return lax.all_to_all(copies, axis, split_axis=0, concat_axis=0, tiled=True)  131 us
    psum x8, blocking collectives, by_axis(): return functools.reduce(lax.psum, axes, array)  124 us
    all_gather x7, blocking collectives, rows_first(): whole = lax.all_gather(both, axis, axis=0, tiled=True)  63 us
    all_to_all x7, blocking collectives, sum_at_owner(): lax.all_to_all(pieces, axis, split_axis=0, concat_axis=0, tiled=True)  45.9 us
    broadcast_in_dim x31, local copies, waits for them, and re-layouts, from_everyone(): copies = jnp.broadcast_to(array, (lax.axis_size(axis), *array.shape))  21 us
  transfers between devices with their start and end apart: 29, of which 29 were waited for; matrix products, arithmetic and copies ran while one was open for 1% of the time, Pallas kernels for 0%

commit v1 on v0

v1 whole, which is shorter than its diff:
```python
import functools

import jax
import jax.numpy as jnp
from jax import lax
from jax.experimental import pallas as pl
from jax.experimental.pallas import tpu as pltpu
from jax.sharding import Mesh
from jax.sharding import PartitionSpec as P

AXES = ("leaf_0", "leaf_1", "leaf_2", "front")
LEAF = AXES[:3]
F32, BF16 = jnp.float32, jnp.bfloat16
MESH = pl.DeviceIdType.MESH
EXACT = lax.Precision.HIGHEST
BATCH, LEAF_CUT, SEP_CUT, COUPLE = 32, 256, 128, 128
LEAF_ROWS, SEP_ROWS, GROUPS = 1024, 512, 64
TOTAL = GROUPS * (LEAF_ROWS + SEP_ROWS)


def nt(a, b):
    return lax.dot_general(a, b, (((1,), (1,)), ((), ())), precision=EXACT, preferred_element_type=F32)


def nn(a, b):
    return lax.dot_general(a, b, (((1,), (0,)), ((), ())), precision=EXACT, preferred_element_type=F32)


def plain(a, b, last):
    return lax.dot_general(a, b, (((1,), (last,)), ((), ())), preferred_element_type=F32)


def split3(a):
    high = a.astype(BF16)
    rest = a - high.astype(F32)
    mid = rest.astype(BF16)
    low = (rest - mid.astype(F32)).astype(BF16)
    return high, mid, low


def select_from(a, chosen, last):
    rows = a.shape[0]
    pieces = plain(jnp.concatenate(split3(a), axis=0), chosen, last)
    return pieces[:rows] + pieces[rows : 2 * rows] + pieces[2 * rows :]


def select_rows(chosen, a):
    high, mid, low = split3(a)
    return plain(chosen, high, 0) + plain(chosen, mid, 0) + plain(chosen, low, 0)


def ones_where(test):
    return jnp.where(test, 1.0, 0.0).astype(BF16)


def iota(shape, dim):
    return lax.broadcasted_iota(jnp.int32, shape, dim)


def kernel(
    rhs_leaf, rhs_sep, inv_leaf, inv_sep, push_leaf, push_sep, pull_leaf, pull_sep,
    rows_leaf, rows_sep, pivot_leaf, pivot_sep, basis_leaf, basis_sep,
    q_leaf, q_sep, coeffs, rfac,
    v_leaf, v_sep, pulls_sep, pulls_leaf, perm_leaf, sums, m_parts, aep, kid_rows,
    u, y, y_leaf, c_out, yk_out, m_full, gn, ls, z, w2s,
    ar_c, ar_x, ar_y, ar_z, br_c, br_x, br_y, br_z,
    front_send, front_recv, tree_send, tree_recv, ar_send, ar_recv,
):
    zi, yi, ci, fi = (lax.axis_index(name) for name in AXES)
    g = zi * 8 + yi * 2 + ci
    low = jnp.int32(1)
    for k in range(1, 7):
        low = low + (1 - (g % 2**k + 2**k - 1) // 2**k) * 2 ** (k - 1)
    nonroot = (g + 63) // 64
    even = 1 - ci
    parent = ((2 * (g // (4 * low)) + 1) * 2 * low) % GROUPS
    upper = (g // (2 * low)) % 2
    kid_low, kid_high = (g + GROUPS - low // 2) % GROUPS, (g + low // 2) % GROUPS

    def at_group(k):
        return (k // 8, (k // 2) % 4, k % 2, fi)

    partner = (zi, yi, 1 - ci, fi)

    def front_peer(i):
        return (zi, yi, ci, (fi + i) % 4)

    barrier = pltpu.get_barrier_semaphore()

    def greet(device):
        pl.semaphore_signal(barrier, inc=1, device_id=device, device_id_type=MESH)

    for i in range(1, 4):
        greet(front_peer(i))
        greet((zi, (yi + i) % 4, ci, fi))
    for i in range(1, 8):
        greet(((zi + i) % 8, yi, ci, fi))
    greet(partner)

    @pl.when(nonroot == 1)
    def _():
        greet(at_group(parent))

    @pl.when(ci == 0)
    def _():
        greet(at_group(kid_low))

    @pl.when(jnp.logical_and(ci == 0, nonroot == 1))
    def _():
        greet(at_group(kid_high))

    pl.semaphore_wait(barrier, 14 + nonroot + even * (1 + nonroot))

    def remote(src, dst, send, recv, device):
        return pltpu.make_async_remote_copy(
            src_ref=src, dst_ref=dst, send_sem=send, recv_sem=recv, device_id=device, device_id_type=MESH
        )

    def to_front(kind, src, slots):
        return [
            remote(src, slots.at[fi], front_send.at[kind, i - 1], front_recv.at[kind, i - 1], front_peer(i))
            for i in range(1, 4)
        ]

    def start(copies):
        for copy in copies:
            copy.start()

    def from_front(kind, slots):
        for i in range(1, 4):
            slot = slots.at[(fi + 4 - i) % 4]
            remote(slot, slot, front_send.at[kind, i - 1], front_recv.at[kind, i - 1], front_peer(i)).wait_recv()

    def edge(kind, src, dst, device, lands=None):
        return remote(src, dst, tree_send.at[kind], tree_recv.at[kind if lands is None else lands], device)

    sent_leaf = to_front(0, rhs_leaf, v_leaf)
    sent_sep = to_front(1, rhs_sep, v_sep)
    start(sent_leaf)
    start(sent_sep)

    def rows_edge(leaf_side, low_side):
        if leaf_side:
            return edge(0, rows_leaf, kid_rows.at[0], partner)
        if low_side:
            return edge(2, rows_sep, kid_rows.at[0], at_group(parent))
        return edge(3, rows_sep, kid_rows.at[1], at_group(parent))

    is_low = jnp.logical_and(nonroot == 1, upper == 0)
    is_high = jnp.logical_and(nonroot == 1, upper == 1)

    @pl.when(ci == 0)
    def _():
        rows_edge(True, True).start()

    @pl.when(is_low)
    def _():
        rows_edge(False, True).start()

    @pl.when(is_high)
    def _():
        rows_edge(False, False).start()

    sent_pull_sep = to_front(2, pull_sep.at[0], pulls_sep)
    sent_pull_leaf = to_front(3, pull_leaf.at[0], pulls_leaf)
    start(sent_pull_sep)
    start(sent_pull_leaf)

    v_leaf[fi] = rhs_leaf[...]
    v_sep[fi] = rhs_sep[...]
    pulls_sep[fi] = pull_sep[0]
    pulls_leaf[fi] = pull_leaf[0]

    pivots = pivot_leaf[...]
    for s in range(4):
        perm_leaf[s * 256 : (s + 1) * 256] = ones_where(iota((256, LEAF_ROWS), 0) + s * 256 == pivots)
    perm_sep = ones_where(iota((SEP_ROWS, SEP_ROWS), 0) == pivot_sep[...])
    from_front(0, v_leaf)
    moved = select_from(v_leaf[0], perm_leaf[0:256], 0)
    for s in range(1, 4):
        moved = moved + select_from(v_leaf[s], perm_leaf[s * 256 : (s + 1) * 256], 0)
    ls[...] = nt(moved, inv_leaf[0])
    from_front(1, v_sep)
    moved = select_from(v_sep[0], perm_sep[0:128], 0)
    for s in range(1, 4):
        moved = moved + select_from(v_sep[s], perm_sep[s * 128 : (s + 1) * 128], 0)
    s0 = nt(moved, inv_sep[0])
    sums[fi, 0:32] = nt(ls[...], push_leaf[0])
    sums[fi, 32:64] = nt(s0, push_sep[0])
    sums[fi, 64:96] = s0
    sent_sums = to_front(4, sums.at[fi], sums)
    start(sent_sums)

    @pl.when(ci == 1)
    def _():
        kid_rows[1] = rows_leaf[...]
        edge(0, rows_leaf, kid_rows.at[0], partner).wait_recv()

    @pl.when(ci == 0)
    def _():
        edge(2, rows_sep, kid_rows.at[0], partner).wait_recv()

    @pl.when(jnp.logical_and(ci == 0, nonroot == 1))
    def _():
        edge(3, rows_sep, kid_rows.at[1], partner).wait_recv()

    @pl.when(nonroot == 0)
    def _():
        kid_rows[1] = jnp.full((1, COUPLE), -1, jnp.int32)
        u[1] = jnp.zeros((BATCH, COUPLE), F32)
        y[...] = jnp.zeros((BATCH, COUPLE), F32)

    columns = [
        jnp.transpose(jnp.broadcast_to(kid_rows[k].astype(F32), (COUPLE, COUPLE))) for k in range(2)
    ]
    pivots_f = pivot_sep[...].astype(F32)

    def wide(column):
        return jnp.concatenate([column] * 4, axis=1)

    picked = jnp.concatenate(
        [ones_where(wide(column) == pivots_f) for column in columns], axis=0
    )
    chosen = jnp.concatenate(
        [ones_where(wide(column) == iota((COUPLE, SEP_ROWS), 1).astype(F32)) for column in columns], axis=0
    )
    ae = select_from(inv_sep[0], picked, 1)
    m_parts[fi] = nn(push_sep[0], ae)
    sent_m = to_front(5, m_parts.at[fi], m_parts)
    start(sent_m)

    from_front(2, pulls_sep)
    moved = select_from(jnp.transpose(pulls_sep[0]), perm_sep[0:128], 0)
    for s in range(1, 4):
        moved = moved + select_from(jnp.transpose(pulls_sep[s]), perm_sep[s * 128 : (s + 1) * 128], 0)
    ap = nt(inv_sep[0], moved)
    aep[fi, :, 0:256] = ae
    aep[fi, :, 256:384] = ap
    sent_aep = to_front(6, aep.at[fi], aep)
    start(sent_aep)

    from_front(4, sums)
    total = ((sums[0] + sums[1]) + sums[2]) + sums[3]
    d = total[32:64]
    c_out[0] = total[0:32]

    @pl.when(ci == 0)
    def _():
        edge(1, c_out.at[0], u.at[0], partner).start()

    from_front(5, m_parts)
    m_full[...] = ((m_parts[0] + m_parts[1]) + m_parts[2]) + m_parts[3]

    def up():
        both = jnp.concatenate([u[0], u[1]], axis=1)
        c_out[1] = d - nt(both, m_full[...])

        @pl.when(is_low)
        def _():
            edge(4, c_out.at[1], u.at[0], at_group(parent)).start()

        @pl.when(is_high)
        def _():
            edge(5, c_out.at[1], u.at[1], at_group(parent)).start()

    @pl.when(ci == 1)
    def _():
        u[1] = c_out[0]
        edge(1, c_out.at[0], u.at[0], partner).wait_recv()
        up()

    from_front(6, aep)
    found = select_rows(chosen[:, 0:128], aep[0])
    for s in range(1, 4):
        found = found + select_rows(chosen[:, s * 128 : (s + 1) * 128], aep[s])
    gn[...] = found
    s0_all = jnp.concatenate([sums[s, 64:96] for s in range(4)], axis=1)
    r = select_from(s0_all, chosen, 1)
    from_front(3, pulls_leaf)
    moved = select_from(jnp.transpose(pulls_leaf[0]), perm_leaf[0:256], 0)
    for s in range(1, 4):
        moved = moved + select_from(jnp.transpose(pulls_leaf[s]), perm_leaf[s * 256 : (s + 1) * 256], 0)
    ap_leaf = nt(inv_leaf[0], moved)

    z[...] = jnp.zeros_like(z)
    z[64:114, 0:256] = basis_leaf[...]
    z[64:114, 256:384] = basis_sep[...]
    w2s[...] = jnp.zeros_like(w2s)

    @pl.when(ci == 0)
    def _():
        edge(4, c_out.at[1], u.at[0], partner).wait_recv()

    @pl.when(jnp.logical_and(ci == 0, nonroot == 1))
    def _():
        edge(5, c_out.at[1], u.at[1], partner).wait_recv()

    @pl.when(ci == 0)
    def _():
        up()

    both = jnp.concatenate([u[0], u[1]], axis=1)
    waiting = r - nt(both, gn[:, 0:256])

    @pl.when(nonroot == 1)
    def _():
        edge(6, yk_out.at[0], y, partner).wait_recv()

    below = waiting - nt(y[...], gn[:, 256:384])
    yk_out[0] = below[:, 0:128]
    yk_out[1] = below[:, 128:256]

    @pl.when(ci == 1)
    def _():
        edge(7, yk_out.at[0], y_leaf, partner).start()
        y_leaf[...] = yk_out[1]

    @pl.when(ci == 0)
    def _():
        edge(6, yk_out.at[0], y, at_group(kid_low)).start()

    @pl.when(jnp.logical_and(ci == 0, nonroot == 1))
    def _():
        edge(8, yk_out.at[1], y, at_group(kid_high), 6).start()

    x_sep = s0 - nt(jnp.concatenate([both, y[...]], axis=1), aep[fi])

    @pl.when(ci == 0)
    def _():
        edge(7, yk_out.at[0], y_leaf, partner).wait_recv()

    x_leaf = ls[...] - nt(y_leaf[...], ap_leaf)
    z[0:32, 0:256] = x_leaf
    z[0:32, 256:384] = x_sep

    sent_sum = []

    def everywhere(first_sem, value, slots):
        places = ((2, ci, lambda k: (zi, yi, k, fi)), (4, fi, lambda k: (zi, yi, ci, k)),
                  (4, yi, lambda k: (zi, k, ci, fi)), (8, zi, lambda k: (k, yi, ci, fi)))
        sem = first_sem
        for (count, mine, device), slot in zip(places, slots):
            slot[mine] = value
            copies = []
            for i in range(1, count):
                copies.append(
                    remote(slot.at[mine], slot.at[mine], ar_send.at[sem + i], ar_recv.at[sem + i],
                           device((mine + i) % count))
                )
                copies[-1].start()
            for i in range(1, count):
                came = slot.at[(mine + count - i) % count]
                remote(came, came, ar_send.at[sem + i], ar_recv.at[sem + i], device((mine + i) % count)).wait_recv()
            sent_sum.extend(copies)
            sem += count
            value = slot[0]
            for k in range(1, count):
                value = value + slot[k]
        return value * (1.0 / TOTAL)

    lane = iota((BATCH, 128), 1)
    row = iota((BATCH, 128), 0)
    w = z[0:32]
    rows_in = jnp.concatenate([w, z[64:128]], axis=0)
    found = everywhere(0, nt(rows_in, z[...]), (ar_c, ar_x, ar_y, ar_z))
    first = jnp.where(lane >= 64, found[0:32], 0.0)
    metric = jnp.concatenate(
        [jnp.zeros((64, 128), F32), jnp.where(iota((64, 128), 1) >= 64, found[32:96], 0.0)], axis=0
    )
    once = w - nn(first, z[...])
    z[0:32] = once
    found = everywhere(18, nt(once, z[...]), (br_c, br_x, br_y, br_z))
    second = jnp.where(lane >= 64, found, 0.0)
    own = jnp.where(lane < 32, found, 0.0)
    second_rows = jnp.concatenate([second, jnp.zeros((96, 128), F32)], axis=0)
    gram = own + nt(nn(second, metric) - 2.0 * second, second_rows)
    w2s[32:64] = once - nn(second, z[...])

    work = gram + jnp.where(lane == row + 32, 1.0, 0.0)
    for j in range(BATCH):
        pivot = work[j : j + 1, j : j + 1]
        root = lax.rsqrt(pivot)
        root = root * (1.5 - 0.5 * pivot * root * root)
        line = work[j : j + 1, :] * root
        column = work[:, j : j + 1] * root
        work = jnp.where(row > j, work - column * line, jnp.where(row == j, line, work))
    q = nn(jnp.where(jnp.logical_and(lane >= 32, lane < 64), work, 0.0), w2s[...])
    q_leaf[...] = q[:, 0:256]
    q_sep[...] = q[:, 256:384]
    rfac[...] = jnp.where(lane >= row, work, 0.0)[:, 0:32]
    coeff = jnp.transpose(jnp.concatenate([first + second, jnp.zeros((96, 128), F32)], axis=0))
    coeffs[...] = coeff[64:114, 0:32]

    for copies in (sent_leaf, sent_sep, sent_pull_sep, sent_pull_leaf, sent_sums, sent_m, sent_aep, sent_sum):
        for copy in copies:
            copy.wait_send()

    @pl.when(ci == 0)
    def _():
        rows_edge(True, True).wait_send()
        edge(1, c_out.at[0], u.at[0], partner).wait_send()
        edge(6, yk_out.at[0], y, partner).wait_send()

    @pl.when(jnp.logical_and(ci == 0, nonroot == 1))
    def _():
        edge(8, yk_out.at[1], y, partner).wait_send()

    @pl.when(ci == 1)
    def _():
        edge(7, yk_out.at[0], y_leaf, partner).wait_send()

    @pl.when(is_low)
    def _():
        rows_edge(False, True).wait_send()
        edge(4, c_out.at[1], u.at[0], partner).wait_send()

    @pl.when(is_high)
    def _():
        rows_edge(False, False).wait_send()
        edge(5, c_out.at[1], u.at[1], partner).wait_send()


def on_device(*arrays):
    vmem = pl.BlockSpec(memory_space=pltpu.VMEM)
    block = pltpu.VMEM((BATCH, COUPLE), F32)

    def shaped(*dims):
        return pltpu.VMEM(dims, F32)

    return pl.pallas_call(
        kernel,
        out_shape=(
            jax.ShapeDtypeStruct((BATCH, LEAF_CUT), F32),
            jax.ShapeDtypeStruct((BATCH, SEP_CUT), F32),
            jax.ShapeDtypeStruct((50, BATCH), F32),
            jax.ShapeDtypeStruct((BATCH, BATCH), F32),
        ),
        in_specs=[vmem] * 14,
        out_specs=(vmem,) * 4,
        scratch_shapes=[
            shaped(4, 32, 256), shaped(4, 32, 128), shaped(4, 128, 128), shaped(4, 256, 128),
            pltpu.VMEM((1024, 1024), BF16), shaped(4, 96, 128), shaped(4, 128, 256), shaped(4, 128, 384),
            pltpu.VMEM((2, 1, 128), jnp.int32),
            shaped(2, 32, 128), block, block, shaped(2, 32, 128), shaped(2, 32, 128),
            shaped(128, 256), shaped(256, 384), shaped(32, 256), shaped(128, 384), shaped(128, 384),
            shaped(2, 96, 128), shaped(4, 96, 128), shaped(4, 96, 128), shaped(8, 96, 128),
            shaped(2, 32, 128), shaped(4, 32, 128), shaped(4, 32, 128), shaped(8, 32, 128),
            pltpu.SemaphoreType.DMA((7, 3)), pltpu.SemaphoreType.DMA((7, 3)),
            pltpu.SemaphoreType.DMA((9,)), pltpu.SemaphoreType.DMA((9,)),
            pltpu.SemaphoreType.DMA((36,)), pltpu.SemaphoreType.DMA((36,)),
        ],
        compiler_params=pltpu.CompilerParams(collective_id=0, has_side_effects=True),
    )(*arrays)


def solution(mesh):
    torus = Mesh(mesh.devices.reshape(8, 4, 2, 4), AXES)
    return jax.shard_map(
        on_device,
        mesh=torus,
        in_specs=(
            P(None, AXES), P(None, AXES),
            P(LEAF, "front", None), P(LEAF, "front", None),
            P(LEAF, None, "front"), P(LEAF, None, "front"),
            P(LEAF, "front", None), P(LEAF, "front", None),
            P(LEAF, None), P(LEAF, None), P(LEAF, None), P(LEAF, None),
            P(None, AXES), P(None, AXES),
        ),
        out_specs=(P(None, AXES), P(None, AXES), P(), P()),
        check_vma=False,
    )
```

time: 976 us -> 133 us (0.14); the launches traced: 962 us -> 132 us
  blocking collectives: 364 us -> 0 us
  waiting for transfers between devices: 326 us -> 0 us
  starting transfers between devices: 167 us -> 0 us
  Pallas kernels: 0 us -> 128 us
  local copies, waits for them, and re-layouts: 50 us -> 3.5 us
  other arithmetic: 40.6 us -> 0 us
  matrix products: 11.6 us -> 0 us
    all_to_all x29 -> x0, waiting for transfers between devices: 326 us -> none  [from_everyone(): return lax.all_to_all(copies, axis, split_axis=0, concat_axis=0, tiled=True)]
    all_to_all x16 -> x0, blocking collectives: 177 us -> none  [the longest x9 131 us: from_everyone(): return lax.all_to_all(copies, axis, split_axis=0, concat_axis=0, tiled=True)]
    all_to_all x29 -> x0, starting transfers between devices: 167 us -> none  [from_everyone(): return lax.all_to_all(copies, axis, split_axis=0, concat_axis=0, tiled=True)]
    pallas_call x0 -> x1, Pallas kernels: none -> 128 us  [on_device(): pl.pallas_call(kernel, out_shape=(jax.ShapeDtypeStruct((BATCH, LEAF_CUT),...]
    psum x8 -> x0, blocking collectives: 124 us -> none  [by_axis(): return functools.reduce(lax.psum, axes, array)]
    all_gather x7 -> x0, blocking collectives: 63 us -> none  [rows_first(): whole = lax.all_gather(both, axis, axis=0, tiled=True)]
    broadcast_in_dim x31 -> x0, local copies, waits for them, and re-layouts: 21 us -> none  [from_everyone(): copies = jnp.broadcast_to(array, (lax.axis_size(axis), *array.shape))]
    scatter-add x14 -> x0, other arithmetic: 18.8 us -> none  [on_device(): dense.at[:, first_rows].add(first_full).at[:, second_rows].add(second_full)]
  transfers between devices with their start and end apart: 29 -> 0, of which waited for: 29 -> 0; matrix products, arithmetic and copies ran while one was open for 1% -> 0% of each run, Pallas kernels for 0% -> 0%
where the time goes in v1:
time: 133 us; the launch traced here: 132 us
  Pallas kernels  128 us (96%)
  local copies, waits for them, and re-layouts  3.5 us (3%)
    pallas_call x1, Pallas kernels, on_device(): pl.pallas_call(kernel, out_shape=(jax.ShapeDtypeStruct((BATCH, LEAF_CUT),...  128 us

profile of v1, /device:TPU:1, one launch (start us, length us, event | category | flops | bytes accessed | tf_op | source)
XLA Modules:
  0.0 132.3 jit_solution(8564247909040292588)
XLA Ops:
  0.6 128.1 %shard_map.165 = (f32[32,256]{1,0:T(8,128)}, f32[32,128]{1,0:T(8,128)}, f32[50,32]{1,0:T(8,128)}, f32[32,32]{1,0:T(8,128)}) custom-call(f32[32,256]{1,0:T(8,128)} %rhs_leaf.1, f32[32,128]{1,0:T(8,128)} %rhs_sep.1, f32[1,256,1024]{2,1,0:T(8,128)} %inv_leaf.1, f32[1,128,512]{2,1,0:T(8,128)} %inv_sep.1, f32[1,128,256]{2,1,0:T(8,128)} %push_leaf.1, ...), custom_call_target="tpu_custom_call" | custom-call | tf_op jit(solution)/shard_map/pallas_call | solution.py:430
  128.8 0.0 copy-start
  128.8 1.4 %copy.18 = f32[50,32]{0,1:T(8,128)} copy(f32[50,32]{1,0:T(8,128)} %get-tuple-element.6) | data formatting | bytes 12800 | tf_op jit(solution)/shard_map/pallas_call | solution.py:430
  130.2 0.0 copy-done
  130.2 0.0 copy-start.2
  130.2 0.6 copy.22
  130.8 0.1 copy-done.2
  131.0 0.0 copy-start.1
  131.0 0.6 copy.23
  131.6 0.1 copy-done.1
  131.7 0.6 copy.24
Async XLA Ops:
  128.8 1.4 %copy-start = (f32[32,256]{1,0:T(8,128)S(1)}, f32[32,256]{1,0:T(8,128)}, u32[]{:S(2)}) copy-start(f32[32,256]{1,0:T(8,128)} %get-tuple-element.12) | copy-start | bytes 98308
  130.2 0.7 copy-start.2
  131.0 0.7 copy-start.1
